TPU v7x, 32 devices: a whole 2x2x4 slice. The times are simulated.
32 devices in a mesh: fit: 4 (over z), pair: 8 (over y, x, core).
Axes of the slice: x: 2, y: 2, z: 4, core: 2. Of those that a mesh axis runs over, the one named last changes fastest.
Arguments:
- metric_factor: bfloat16 [4096, 4096], P('fit'), as said below
- three_index: bfloat16 [4096, 16384], P('fit', 'pair'), may hold values from -6 to 6
- send_map: int32 [8, 8, 16], P('pair'), may hold values from 0 to 15
- pair_slots: int32 [8, 128], P('pair'), may hold values from 0 to 127, each once within a row
- pair_count: int32 [8], P('pair'), may hold values from 1 to 64, 256 in all
- orbital_energy: bfloat16 [128], P('pair'), may hold values from -2 to -0.19921875
- cabs_energy: float32 [1024], replicated, may hold values from 0.5 to 4
- coupling: bfloat16 [128, 1024], replicated, may hold values from -0.5 to 0.5
Outputs:
- projected: bfloat16 [8, 64, 128, 1024], P('pair', 'fit')
Inputs may be any that keep to these rules, and one draw needn't show every extreme that they name: `metric_factor`: diagonal entries lie between 0.6 and 1.4. `pair_slots`: each row holds every position 0 to 127 once; pair n of a row uses entries 2n and 2n + 1.
All inputs are finite; a program needn't handle non-finite values. No bound on the sum of `pair_count` on one device may be relied on, other than what follows from the above.
Results may differ from a plain program's by a relative error of at most 0.015.
Values may be sent and summed in bfloat16 or wider, within the bound.
No kernel may reach another device: no remote copies, remote signals or barrier semaphores. Data moves between devices by JAX's collectives and lax.ppermute only.
A program may use at most 256 MiB of HBM per device.

v0:
```python
import jax
import jax.numpy as jnp
from jax import lax
from jax.sharding import PartitionSpec as P

NAUX = 4096
PAIR_BLOCK = 8


def on_device(
    metric_factor,
    three_index,
    send_map,
    pair_slots,
    pair_count,
    orbital_energy,
    cabs_energy,
    coupling,
):
    domain = coupling.shape[0]
    orbitals = orbital_energy.shape[0]
    local_rows = metric_factor.shape[0]
    peers = send_map.shape[1]
    capacity = send_map.shape[2]
    slot_total = pair_slots.shape[1] // 2
    fitted = jnp.dot(
        metric_factor,
        lax.all_gather(three_index, "fit", axis=0, tiled=True),
        preferred_element_type=jnp.float32,
    )
    fitted = fitted.astype(jnp.bfloat16).reshape(local_rows, orbitals, domain)
    requests = send_map.reshape(peers, capacity)
    source, energy_src = (
        lax.all_gather(fitted, "pair", axis=1, tiled=True),
        lax.all_gather(orbital_energy, "pair", axis=0, tiled=True),
    )
    global_ids = (jnp.arange(peers, dtype=jnp.int32)[:, None] * orbitals + requests).reshape(-1)
    pair_index = jnp.take(global_ids, pair_slots[0])
    left_index = pair_index[0::2]
    right_index = pair_index[1::2]
    live_count = pair_count[0]
    norm_scale = NAUX ** (-0.5)
    block_count = (live_count + PAIR_BLOCK - 1) // PAIR_BLOCK

    def advance(block, partial_value):
        left_ids = lax.dynamic_slice_in_dim(left_index, block * PAIR_BLOCK, PAIR_BLOCK)
        right_ids = lax.dynamic_slice_in_dim(right_index, block * PAIR_BLOCK, PAIR_BLOCK)
        left_rows = jnp.take(source, left_ids, axis=1)
        right_rows = jnp.take(source, right_ids, axis=1)
        product = jnp.einsum(
            "qsa,qsb->sab", left_rows, right_rows, preferred_element_type=jnp.float32
        )
        return lax.dynamic_update_slice_in_dim(
            partial_value, product * norm_scale, block * PAIR_BLOCK, 0
        )

    partial_value = jnp.zeros((slot_total, domain, domain), jnp.float32)
    partial_value = lax.fori_loop(0, block_count, advance, partial_value)
    share = slot_total // lax.axis_size("fit")
    first_slot = lax.axis_index("fit") * share
    totals = lax.psum(partial_value.astype(jnp.bfloat16), "fit").astype(jnp.float32)
    exchange = lax.dynamic_slice_in_dim(totals, first_slot, share, 0)
    energy_sum = jnp.take(energy_src, left_index).astype(jnp.float32) + jnp.take(
        energy_src, right_index
    ).astype(jnp.float32)
    energy_sum = lax.dynamic_slice_in_dim(energy_sum, first_slot, share, 0)
    weighted = jnp.einsum(
        "sab,bc->sac", exchange.astype(jnp.bfloat16), coupling, preferred_element_type=jnp.float32
    )
    denom = cabs_energy[None, None, :] - energy_sum[:, None, None]
    live_mask = first_slot + jnp.arange(share, dtype=jnp.int32) < live_count
    projected = jnp.where(live_mask[:, None, None], weighted / denom, 0.0).astype(jnp.bfloat16)
    return projected.reshape(1, share, domain, weighted.shape[2])


def solution(mesh):
    in_specs = (
        P("fit", None),
        P("fit", "pair"),
        P("pair", None, None),
        P("pair", None),
        P("pair"),
        P("pair"),
        P(),
        P(),
    )
    out_specs = P("pair", "fit", None, None)
    return jax.shard_map(
        on_device, mesh=mesh, in_specs=in_specs, out_specs=out_specs, check_vma=False
    )
```

profile of v0, /device:TPU:0, one launch (start us, length us, event | category | flops | bytes accessed | tf_op | source)
XLA Modules:
  0.0 655.7 jit_solution(15301180865822851365)
XLA Ops:
  6.5 0.0 copy-start
  6.5 0.0 all-gather.3.cloned.1.call-start
  6.5 0.7 all-gather.3.cloned.1.call-update
  7.3 0.0 all-gather.5.cloned.1.call-start
  7.3 291.1 %all-gather.3.cloned.1.call-done = bf16[4096,2048]{1,0:T(8,128)(2,1)} async-done(((bf16[1024,2048]{1,0:T(8,128)(2,1)}), bf16[4096,2048]{1,0:T(8,128)(2,1)}) %all-gather.3.cloned.1.call-update) | async-done | bytes 16777232 | tf_op jit(solution)/shard_map/all_gather | solution.py:28
  298.4 22.7 %convert_bitcast_fusion = bf16[128,16,8,128]{3,2,1,0:T(8,128)(2,1)S(1)} fusion(bf16[1024,4096]{1,0:T(8,128)(2,1)} %param.14, bf16[4096,2048]{1,0:T(8,128)(2,1)} %all-gather.3.cloned.1.call-done), kind=kOutput, calls=%fused_computation.24 | convolution fusion | flops 17181966336 | bytes 29360128 | tf_op jit(solution)/shard_map/dot_general | solution.py:26
  321.1 3.1 copy.18
  324.2 0.0 copy-start.2
  324.2 0.0 copy-start.3
  324.2 0.0 all-gather.5.cloned.1.call-update
  324.2 0.0 all-reduce.3.cloned.1.call-start
  325.0 0.1 add.77
  325.0 0.1 add.78
  325.1 0.0 copy-done.2
  325.1 0.1 reshape.94
  325.2 0.0 copy-done.3
  325.2 1.2 gather_fusion.2
  326.5 0.2 slice.6
  326.6 0.2 slice.7
  326.8 156.4 %all-gather.5.cloned.1.call-done = bf16[1024,128,128]{2,0,1:T(8,128)(2,1)} async-done(((bf16[1024,16,128]{2,0,1:T(8,128)(2,1)}), bf16[1024,128,128]{2,0,1:T(8,128)(2,1)}) %all-gather.5.cloned.1.call-update) | async-done | bytes 33554448 | tf_op jit(solution)/shard_map/all_gather | solution.py:34
  483.2 1.8 broadcast_in_dim.41
  485.1 27.6 %while.10 = (s32[]{:T(128)}, bf16[64,128,128]{2,1,0:T(8,128)(2,1)}, s32[]{:T(128)}, s32[64]{0:T(128)S(1)}, bf16[1024,128,128]{2,0,1:T(8,128)(2,1)}, /*index=5*/s...) while((s32[]{:T(128)}, bf16[64,128,128]{2,1,0:T(8,128)(2,1)}, s32[]{:T(128)}, s32[64]{0:T(128)S(1)}, ...), condition=%wide.region_1.3_spmd, body=%wide.region_0.0_spmd.sunk | while | flops 270665824 | bytes 13115835 | solution.py:58
  485.1 0.1 compare_and_fusion.3
  485.2 2.3 gather_fusion
  487.5 3.5 gather_fusion.1
  491.0 3.2 fusion.31
  494.2 0.1 compare_and_fusion.3
  494.3 2.3 gather_fusion
  496.7 3.5 gather_fusion.1
  500.2 3.2 fusion.31
  503.4 0.1 compare_and_fusion.3
  503.5 2.3 gather_fusion
  505.9 3.5 gather_fusion.1
  509.4 3.2 fusion.31
  512.6 0.0 all-reduce.3.cloned.1.call-update
  512.7 0.6 copy-done.5
  513.3 0.6 dynamic-slice
  514.6 0.0 copy-done.4
  514.6 0.2 dynamic-update-slice
  514.9 57.0 %all-reduce = bf16[128]{0:T(256)(128)(2,1)S(1)} all-reduce(bf16[128]{0:T(256)(128)(2,1)S(1)} %dynamic-update-slice), channel_id=1, replica_groups=mesh['fit'=4,'pair'=8] {'pair'}, use_global_device_ids=true, to_apply=%add | all-reduce | flops 128 | bytes 512
  571.9 0.8 gather_fusion.3
  572.7 0.8 gather_fusion.4
  573.4 0.1 dynamic_slice.13
  573.5 0.0 copy-done.1
  573.5 0.1 broadcast_subtract_fusion
  573.6 71.3 %all-reduce.3.cloned.1.call-done = bf16[64,128,128]{2,1,0:T(8,128)(2,1)} async-done(((bf16[64,128,128]{2,1,0:T(8,128)(2,1)}), bf16[64,128,128]{2,1,0:T(8,128)(2,1)}) %all-reduce.3.cloned.1.call-update) | async-done | bytes 2097168 | tf_op jit(solution)/shard_map/psum | solution.py:61
  644.9 0.0 copy-done
  644.9 4.3 fusion.19
  (21 shorter events, 0.1 us)
Async XLA Ops:
  6.5 638.3 %copy-start = (bf16[128,1024]{1,0:T(8,128)(2,1)S(1)}, bf16[128,1024]{1,0:T(8,128)(2,1)}, u32[]{:S(2)}) copy-start(bf16[128,1024]{1,0:T(8,128)(2,1)} %param.21) | copy-start | bytes 786436
  6.5 291.9 %all-gather.3.cloned.1.call-start = ((), (), s32[]{:S(2)}) async-start(), calls=%async_computation | async-start | bytes 20971520 | tf_op jit(solution)/shard_map/all_gather | solution.py:28
  7.3 476.0 %all-gather.5.cloned.1.call-start = ((), (), s32[]{:S(2)}) async-start(), calls=%async_computation.1 | async-start | bytes 37748736 | tf_op jit(solution)/shard_map/all_gather | solution.py:34
  324.2 0.9 copy-start.2
  324.2 1.0 copy-start.3
  324.2 320.6 %all-reduce.3.cloned.1.call-start = ((), (), s32[]{:S(2)}) async-start(), calls=%async_computation.2 | async-start | bytes 4194304 | tf_op jit(solution)/shard_map/psum | solution.py:61
  512.6 0.7 copy-start.5
  512.6 2.0 copy-start.4
  512.6 60.9 %copy-start.1 = (f32[1024]{0:T(1024)S(1)}, f32[1024]{0:T(1024)}, u32[]{:S(2)}) copy-start(f32[1024]{0:T(1024)} %param.20) | copy-start | bytes 12292
Sparse Core Ops, SparseCore 0:
  8.9 289.4 all-gather.2
  324.4 158.8 all-gather.4
  512.8 132.0 all-reduce.2
where the time goes:
time: 657 us; the launch traced here: 656 us
  waiting for transfers between devices  520 us (79%)
  blocking collectives  57 us (9%)
  matrix products  36.7 us (6%)
  local copies, waits for them, and re-layouts  27.4 us (4%)
  between operations  14.6 us (2%)
    all_gather x1, waiting for transfers between devices, on_device(): lax.all_gather(three_index, 'fit', axis=0, tiled=True)  291 us
    all_gather x1, waiting for transfers between devices, on_device(): lax.all_gather(fitted, 'pair', axis=1, tiled=True)  156 us
    psum x1, waiting for transfers between devices, on_device(): lax.psum(partial_value.astype(jnp.bfloat16), 'fit').astype(jnp.float32)  71.3 us
    unnamed x1, blocking collectives  57 us
    dot_general x1, matrix products, on_device(): jnp.dot(metric_factor, lax.all_gather(three_index, 'fit', axis=0, tiled=T...  22.7 us
  transfers between devices with their start and end apart: 3, of which 3 were waited for; matrix products, arithmetic and copies ran while one was open for 1% of the time, Pallas kernels for 0%

commit v1 on v0

v1 whole, which is shorter than its diff:
```python
import functools

import jax
import jax.numpy as jnp
from jax import lax
from jax.experimental import pallas as pl
from jax.experimental.pallas import tpu as pltpu
from jax.sharding import PartitionSpec as P


CHUNKS = 4
GROUP = 4


def pair_kernel(n_src, scale, meta_ref, loc_ref, *refs):
    sources = refs[:n_src]
    out_ref = refs[n_src]
    left, right, left_sem, right_sem = refs[n_src + 1 :]
    size = out_ref.shape[1]
    base, groups = meta_ref[0], meta_ref[1]

    def fetch(slot, row, buf, sem, place):
        where = loc_ref[row, slot]
        first = pl.multiple_of(loc_ref[row + 1, slot] * size, size)
        for at, source in enumerate(sources):

            @pl.when(where == at)
            def _():
                pltpu.make_async_copy(
                    source.at[pl.ds(first, size), :], buf.at[place], sem.at[place]
                ).start()

    def fetch_group(group):
        for u in range(GROUP):
            slot = base + group * GROUP + u
            place = lax.rem(group, 2) * GROUP + u
            fetch(slot, 0, left, left_sem, place)
            fetch(slot, 2, right, right_sem, place)

    out_ref[...] = jnp.zeros_like(out_ref)

    @pl.when(groups > 0)
    def _():
        fetch_group(0)

    def advance(group, carry):
        @pl.when(group + 1 < groups)
        def _():
            fetch_group(group + 1)

        first = lax.rem(group, 2) * GROUP
        for u in range(GROUP):
            for buf, sem in ((left, left_sem), (right, right_sem)):
                pltpu.make_async_copy(
                    sources[0].at[pl.ds(0, size), :], buf.at[first + u], sem.at[first + u]
                ).wait()
        for u in range(GROUP):
            product = lax.dot_general(
                left[first + u],
                right[first + u],
                (((1,), (1,)), ((), ())),
                preferred_element_type=jnp.float32,
            )
            out_ref[group * GROUP + u] = (product * scale).astype(out_ref.dtype)
        return carry

    lax.fori_loop(0, groups, advance, 0)


def pair_blocks(sources, meta, loc, share, domain, scale):
    rows = sources[0].shape[1]
    return pl.pallas_call(
        functools.partial(pair_kernel, len(sources), scale),
        out_shape=jax.ShapeDtypeStruct((share, domain, domain), jnp.bfloat16),
        in_specs=[pl.BlockSpec(memory_space=pltpu.SMEM)] * 2
        + [pl.BlockSpec(memory_space=pl.ANY)] * len(sources),
        out_specs=pl.BlockSpec(memory_space=pltpu.VMEM),
        scratch_shapes=[
            pltpu.VMEM((2 * GROUP, domain, rows), jnp.bfloat16),
            pltpu.VMEM((2 * GROUP, domain, rows), jnp.bfloat16),
            pltpu.SemaphoreType.DMA((2 * GROUP,)),
            pltpu.SemaphoreType.DMA((2 * GROUP,)),
        ],
        name="pair_blocks",
    )(meta, loc, *sources)


def times(panel, factor):
    return lax.dot_general(
        panel, factor, (((0,), (1,)), ((), ())), preferred_element_type=jnp.float32
    ).astype(jnp.bfloat16)


def fit_through_hubs(factor, pieces):
    me = lax.axis_index("fit")
    rows = factor.shape[0]
    lane = lax.axis_index("pair")
    slab = rows // lax.axis_size("pair")
    inward, inner, outward = [(0, 1), (3, 2)], [(1, 2), (2, 1)], [(1, 0), (2, 3)]
    is_hub = (me == 1) | (me == 2)
    order = jnp.array([[0, 0, 0, 0], [1, 0, 2, 3], [2, 3, 1, 0], [0, 0, 0, 0]], jnp.int32)[me]

    def blocks(matrix):
        parts = [lax.dynamic_slice_in_dim(matrix, order[i] * rows, rows, 1) for i in range(4)]
        return lax.optimization_barrier(jnp.concatenate(parts, axis=1))

    part = lax.dynamic_slice_in_dim(factor, lane * slab, slab, 0)
    part = lax.ppermute(part, "fit", inward)
    part = lax.optimization_barrier(jnp.where(is_hub, part, jnp.zeros_like(part)))
    served = lax.all_gather(part, "pair", axis=0, tiled=True)
    own_blocks = blocks(factor)
    served_blocks = blocks(served)
    fitted = []
    for piece in pieces:
        outer = lax.ppermute(piece, "fit", inward)
        near = lax.ppermute(piece, "fit", inner)
        far = lax.ppermute(outer, "fit", inner)
        panel = jnp.concatenate([piece, outer, near, far], axis=0)
        panel = lax.optimization_barrier(panel)
        end = lax.optimization_barrier(times(panel, served_blocks))
        given = lax.ppermute(end, "fit", outward)
        own = lax.optimization_barrier(times(panel, own_blocks))
        fitted.append(lax.optimization_barrier(jnp.where(is_hub, own, given)))
    return fitted


def fit_gathered(factor, pieces):
    return [times(lax.all_gather(piece, "fit", axis=0, tiled=True), factor) for piece in pieces]


def on_device(
    metric_factor,
    three_index,
    send_map,
    pair_slots,
    pair_count,
    orbital_energy,
    cabs_energy,
    coupling,
):
    domain = coupling.shape[0]
    orbitals = orbital_energy.shape[0]
    peers = send_map.shape[1]
    capacity = send_map.shape[2]
    slot_total = pair_slots.shape[1] // 2
    fit_size = lax.axis_size("fit")
    me = lax.axis_index("fit")
    share = slot_total // fit_size
    first_slot = me * share
    live_count = pair_count[0]
    scale = metric_factor.shape[1] ** (-0.5)
    group = orbitals // CHUNKS
    width = group * domain

    energy_src = lax.all_gather(orbital_energy, "pair", axis=0, tiled=True)
    peer_ids = jnp.broadcast_to(jnp.arange(peers, dtype=jnp.int32)[:, None], (peers, capacity))
    requests = send_map.reshape(peers, capacity)
    slots = pair_slots[0]
    picked = jnp.take(requests.reshape(-1), slots)
    origin = jnp.take(peer_ids.reshape(-1), slots)
    piece_of = picked // group
    row_of = origin * group + picked % group
    loc = jnp.stack([piece_of[0::2], row_of[0::2], piece_of[1::2], row_of[1::2]])
    energies = jnp.take(energy_src, origin * orbitals + picked).astype(jnp.float32)
    energy_sum = energies[0::2] + energies[1::2]
    energy_sum = lax.dynamic_slice_in_dim(energy_sum, first_slot, share, 0)
    loc, energy_sum = lax.optimization_barrier((loc, energy_sum))

    pieces = [three_index[:, c * width : (c + 1) * width] for c in range(CHUNKS)]
    fit = fit_through_hubs if fit_size == 4 else fit_gathered
    fitted = fit(metric_factor, pieces)
    sources = [lax.all_gather(block, "pair", axis=0, tiled=True) for block in fitted]

    def block_for(target):
        base = target * share
        live = jnp.clip(live_count - base, 0, share)
        meta = jnp.stack([base, (live + GROUP - 1) // GROUP]).astype(jnp.int32)
        return pair_blocks(sources, meta, loc, share, domain, scale)

    received = []
    for shift in sorted(range(1, fit_size), key=lambda d: abs(d - fit_size / 2)):
        block = block_for((me + shift) % fit_size)
        ring = [(i, (i + shift) % fit_size) for i in range(fit_size)]
        received.append(lax.ppermute(block, "fit", ring))
    total = block_for(me).astype(jnp.float32)
    for block in received:
        total = total + block.astype(jnp.float32)
    exchange = total.astype(jnp.bfloat16)

    weighted = jnp.einsum("sab,bc->sac", exchange, coupling, preferred_element_type=jnp.float32)
    denom = cabs_energy[None, None, :] - energy_sum[:, None, None]
    live_mask = first_slot + jnp.arange(share, dtype=jnp.int32) < live_count
    projected = jnp.where(live_mask[:, None, None], weighted / denom, 0.0).astype(jnp.bfloat16)
    return projected.reshape(1, share, domain, weighted.shape[2])


def solution(mesh):
    in_specs = (
        P("fit", None),
        P("fit", "pair"),
        P("pair", None, None),
        P("pair", None),
        P("pair"),
        P("pair"),
        P(),
        P(),
    )
    out_specs = P("pair", "fit", None, None)

    return jax.shard_map(
        on_device, mesh=mesh, in_specs=in_specs, out_specs=out_specs, check_vma=False
    )
```

time: 657 us -> 498 us (0.76)
  the two profiles are of different devices: /device:TPU:0 before, /device:TPU:18 now
where the time goes in v1:
time: 498 us; the launch traced here: 490 us
  waiting for transfers between devices  304 us (61%)
  matrix products  54.1 us (11%)
  starting transfers between devices  41.5 us (8%)
  local copies, waits for them, and re-layouts  21.3 us (4%)
  Pallas kernels  21.2 us (4%)
  other arithmetic  19.2 us (4%)
  between operations  17.9 us (4%)
  blocking collectives  10.8 us (2%)
    ppermute x4, waiting for transfers between devices, fit_through_hubs(): outer = lax.ppermute(piece, 'fit', inward)  79.4 us
    ppermute x4, waiting for transfers between devices, fit_through_hubs(): far = lax.ppermute(outer, 'fit', inner)  78.8 us
    ppermute x4, waiting for transfers between devices, fit_through_hubs(): given = lax.ppermute(end, 'fit', outward)  58.9 us
    dot_general x8, matrix products, times(): lax.dot_general(panel, factor, (((0,), (1,)), ((), ())), preferred_elemen...  49.8 us
    all_gather x4, waiting for transfers between devices, on_device(): lax.all_gather(block, 'pair', axis=0, tiled=True)  35.6 us
    ppermute x3, waiting for transfers between devices, on_device(): received.append(lax.ppermute(block, 'fit', ring))  25.6 us
    ppermute x1, waiting for transfers between devices, fit_through_hubs(): part = lax.ppermute(part, 'fit', inward)  25.5 us
    pallas_call x4, Pallas kernels, pair_blocks(): pl.pallas_call(functools.partial(pair_kernel, len(sources), scale), out_s...  21.2 us
  transfers between devices with their start and end apart: 25, of which 17 were waited for; matrix products, arithmetic and copies ran while one was open for 14% of the time, Pallas kernels for 3%

profile of v1, /device:TPU:18, one launch (start us, length us, event | category | flops | bytes accessed | tf_op | source)
XLA Modules:
  0.0 490.4 jit_solution(5896406329984404962)
XLA Ops:
  9.2 25.5 %collective-permute-done.3 = bf16[128,4096]{1,0:T(8,128)(2,1)S(1)} collective-permute-done((bf16[128,4096]{1,0:T(8,128)(2,1)S(1)}, bf16[128,4096]{1,0:T(8,128)(2,1)S(1)}, u32[]{:S(2)}, u32[]{:S(2)}) %collective-permute-start.3) | collective-permute-done | bytes 1048608 | tf_op jit(solution)/shard_map/ppermute | solution.py:108
  35.8 3.8 fusion.4
  40.9 2.4 collective-permute-start.14
  47.2 18.4 %collective-permute-done.13 = bf16[1024,512]{1,0:T(8,128)(2,1)} collective-permute-done((bf16[1024,512]{1,0:T(8,128)(2,1)S(1)}, bf16[1024,512]{1,0:T(8,128)(2,1)}, u32[]{:S(2)}, u32[]{:S(2)}) %collective-permute-start.13) | collective-permute-done | bytes 1048608 | tf_op jit(solution)/shard_map/ppermute | solution.py:115
  65.7 2.3 collective-permute-start.15
  68.0 4.5 constant_dynamic-slice_fusion.8
  72.5 3.7 pad_maximum_fusion
  76.2 14.7 %collective-permute-done.15 = bf16[1024,512]{1,0:T(8,128)(2,1)S(1)} collective-permute-done((bf16[1024,512]{1,0:T(8,128)(2,1)}, bf16[1024,512]{1,0:T(8,128)(2,1)S(1)}, u32[]{:S(2)}, u32[]{:S(2)}) %collective-permute-start.15) | collective-permute-done | bytes 1048608 | tf_op jit(solution)/shard_map/ppermute | solution.py:117
  90.9 3.3 pad_maximum_fusion.5
  94.3 4.5 constant_dynamic-slice_fusion.3
  99.6 11.2 %convolution_convert_fusion = bf16[512,1024]{1,0:T(8,128)(2,1)} fusion(bf16[4096,512]{1,0:T(8,128)(2,1)} %pad_maximum_fusion.5, bf16[1024,4096]{1,0:T(8,128)(2,1)S(1)} %pad_maximum_fusion.1), kind=kOutput, calls=%fused_computation.11 | convolution fusion | flops 4295491584 | bytes 13631488 | tf_op jit(solution)/shard_map/dot_general | solution.py:89
  110.8 2.4 collective-permute-start.16
  113.3 4.5 convolution_convert_fusion.1
  117.9 15.9 %collective-permute-done.16 = bf16[512,1024]{1,0:T(8,128)(2,1)} collective-permute-done((bf16[512,1024]{1,0:T(8,128)(2,1)}, bf16[512,1024]{1,0:T(8,128)(2,1)}, u32[]{:S(2)}, u32[]{:S(2)}) %collective-permute-start.16) | collective-permute-done | bytes 1048608 | tf_op jit(solution)/shard_map/ppermute | solution.py:121
  136.6 2.2 collective-permute-start.10
  138.8 22.9 %collective-permute-done.9 = bf16[1024,512]{1,0:T(8,128)(2,1)S(1)} collective-permute-done((bf16[1024,512]{1,0:T(8,128)(2,1)}, bf16[1024,512]{1,0:T(8,128)(2,1)S(1)}, u32[]{:S(2)}, u32[]{:S(2)}) %collective-permute-start.9) | collective-permute-done | bytes 1048608 | tf_op jit(solution)/shard_map/ppermute | solution.py:115
  161.7 1.9 collective-permute-start.11
  163.6 22.5 %collective-permute-done.11 = bf16[1024,512]{1,0:T(8,128)(2,1)S(1)} collective-permute-done((bf16[1024,512]{1,0:T(8,128)(2,1)S(1)}, bf16[1024,512]{1,0:T(8,128)(2,1)S(1)}, u32[]{:S(2)}, u32[]{:S(2)}) %collective-permute-start.11) | collective-permute-done | bytes 1048608 | tf_op jit(solution)/shard_map/ppermute | solution.py:117
  187.7 5.5 %convolution_convert_fusion.2 = bf16[512,1024]{1,0:T(8,128)(2,1)} fusion(bf16[4096,512]{1,0:T(8,128)(2,1)S(1)} %pad_maximum_fusion.4, bf16[1024,4096]{1,0:T(8,128)(2,1)S(1)} %copy-done.2), kind=kOutput, calls=%fused_computation.13 | convolution fusion | flops 4295491584 | bytes 13631488 | tf_op jit(solution)/shard_map/dot_general | solution.py:89
  193.2 1.6 collective-permute-start.12
  194.8 4.5 convolution_convert_fusion.3
  199.3 15.0 %collective-permute-done.12 = bf16[512,1024]{1,0:T(8,128)(2,1)S(1)} collective-permute-done((bf16[512,1024]{1,0:T(8,128)(2,1)}, bf16[512,1024]{1,0:T(8,128)(2,1)S(1)}, u32[]{:S(2)}, u32[]{:S(2)}) %collective-permute-start.12) | collective-permute-done | bytes 1048608 | tf_op jit(solution)/shard_map/ppermute | solution.py:121
  216.8 2.5 collective-permute-start.6
  219.3 19.5 %collective-permute-done.5 = bf16[1024,512]{1,0:T(8,128)(2,1)S(1)} collective-permute-done((bf16[1024,512]{1,0:T(8,128)(2,1)}, bf16[1024,512]{1,0:T(8,128)(2,1)S(1)}, u32[]{:S(2)}, u32[]{:S(2)}) %collective-permute-start.5) | collective-permute-done | bytes 1048608 | tf_op jit(solution)/shard_map/ppermute | solution.py:115
  238.8 2.7 collective-permute-start.7
  241.6 21.0 %collective-permute-done.7 = bf16[1024,512]{1,0:T(8,128)(2,1)S(1)} collective-permute-done((bf16[1024,512]{1,0:T(8,128)(2,1)S(1)}, bf16[1024,512]{1,0:T(8,128)(2,1)S(1)}, u32[]{:S(2)}, u32[]{:S(2)}) %collective-permute-start.7) | collective-permute-done | bytes 1048608 | tf_op jit(solution)/shard_map/ppermute | solution.py:117
  264.1 7.4 %convolution_convert_fusion.4 = bf16[512,1024]{1,0:T(8,128)(2,1)S(1)} fusion(bf16[4096,512]{1,0:T(8,128)(2,1)S(1)} %pad_maximum_fusion.3, bf16[1024,4096]{1,0:T(8,128)(2,1)} %copy-done.1), kind=kOutput, calls=%fused_computation.15 | convolution fusion | flops 4295491584 | bytes 13631488 | tf_op jit(solution)/shard_map/dot_general | solution.py:89
  271.5 1.8 collective-permute-start.8
  273.3 4.5 convolution_convert_fusion.5
  277.9 13.9 %collective-permute-done.8 = bf16[512,1024]{1,0:T(8,128)(2,1)S(1)} collective-permute-done((bf16[512,1024]{1,0:T(8,128)(2,1)S(1)}, bf16[512,1024]{1,0:T(8,128)(2,1)S(1)}, u32[]{:S(2)}, u32[]{:S(2)}) %collective-permute-start.8) | collective-permute-done | bytes 1048608 | tf_op jit(solution)/shard_map/ppermute | solution.py:121
  294.2 2.7 collective-permute-start.1
  296.9 18.6 %collective-permute-done = bf16[1024,512]{1,0:T(8,128)(2,1)S(1)} collective-permute-done((bf16[1024,512]{1,0:T(8,128)(2,1)S(1)}, bf16[1024,512]{1,0:T(8,128)(2,1)S(1)}, u32[]{:S(2)}, u32[]{:S(2)}) %collective-permute-start) | collective-permute-done | bytes 1048608 | tf_op jit(solution)/shard_map/ppermute | solution.py:115
  315.5 2.7 collective-permute-start.2
  318.5 20.6 %collective-permute-done.2 = bf16[1024,512]{1,0:T(8,128)(2,1)S(1)} collective-permute-done((bf16[1024,512]{1,0:T(8,128)(2,1)S(1)}, bf16[1024,512]{1,0:T(8,128)(2,1)S(1)}, u32[]{:S(2)}, u32[]{:S(2)}) %collective-permute-start.2) | collective-permute-done | bytes 1048608 | tf_op jit(solution)/shard_map/ppermute | solution.py:117
  339.4 7.4 %convolution_convert_fusion.6 = bf16[512,1024]{1,0:T(8,128)(2,1)S(1)} fusion(bf16[4096,512]{1,0:T(8,128)(2,1)S(1)} %pad_maximum_fusion.2, bf16[1024,4096]{1,0:T(8,128)(2,1)} %copy-done.1), kind=kOutput, calls=%fused_computation.17 | convolution fusion | flops 4295491584 | bytes 13631488 | tf_op jit(solution)/shard_map/dot_general | solution.py:89
  346.9 1.7 collective-permute-start.4
  348.6 4.5 convolution_convert_fusion.7
  353.2 14.1 %collective-permute-done.4 = bf16[512,1024]{1,0:T(8,128)(2,1)S(1)} collective-permute-done((bf16[512,1024]{1,0:T(8,128)(2,1)S(1)}, bf16[512,1024]{1,0:T(8,128)(2,1)S(1)}, u32[]{:S(2)}, u32[]{:S(2)}) %collective-permute-start.4) | collective-permute-done | bytes 1048608 | tf_op jit(solution)/shard_map/ppermute | solution.py:121
  373.9 10.8 %all-reduce = bf16[128]{0:T(256)(128)(2,1)S(1)} all-reduce(bf16[128]{0:T(256)(128)(2,1)S(1)} %dynamic-update-slice), channel_id=1, replica_groups=mesh['fit'=4,'pair'=8] {'pair'}, use_global_device_ids=true, to_apply=%add | all-reduce | flops 128 | bytes 512
  388.3 35.6 %all-gather.8.cloned.1.call-done.refs_0_ = bf16[4096,1024]{1,0:T(8,128)(2,1)} async-done(((bf16[512,1024]{1,0:T(8,128)(2,1)}), bf16[4096,1024]{1,0:T(8,128)(2,1)}) %all-gather.8.cloned.1.call-update) | async-done | bytes 8388624 | tf_op jit(solution)/shard_map/all_gather | solution.py:172
  423.9 6.7 %pair_blocks.5 = bf16[16,128,128]{2,1,0:T(8,128)(2,1)} custom-call(s32[2]{0:T(128)} %get-tuple-element.29.meta_ref, s32[4,64]{1,0:T(4,128)} %pad_add_fusion.loc_ref, bf16[4096,1024]{1,0:T(8,128)(2,1)} %all-gather.8.cloned.1.call-done.refs_0_, bf16[4096,1024]{1,0:T(8,128)(2,1)} %all-gather.10.cloned.1.call-done.refs_1_, ...), custom_call_target="tpu_custom_call" | custom-call | tf_op jit(solution)/shard_map/pair_blocks/pallas_call | solution.py:72
  430.9 1.7 pair_blocks.6
  432.6 6.0 %collective-permute-start.18 = (bf16[16,128,128]{2,1,0:T(8,128)(2,1)}, bf16[16,128,128]{2,1,0:T(8,128)(2,1)S(1)}, u32[]{:S(2)}, u32[]{:S(2)}) collective-permute-start(bf16[16,128,128]{2,1,0:T(8,128)(2,1)} %pair_blocks.6), channel_id=1, source_target_pairs={{0,8},{8,16},{16,24},{24,0},{1,9},{9,17},{17,25},{25,1},{2,10},{10... | collective-permute-start | bytes 1572872 | tf_op jit(solution)/shard_map/ppermute | solution.py:184
  438.6 6.4 %pair_blocks.7 = bf16[16,128,128]{2,1,0:T(8,128)(2,1)} custom-call(s32[2]{0:T(128)} %pad_add_fusion.4.meta_ref, s32[4,64]{1,0:T(4,128)} %pad_add_fusion.loc_ref, bf16[4096,1024]{1,0:T(8,128)(2,1)} %all-gather.8.cloned.1.call-done.refs_0_, bf16[4096,1024]{1,0:T(8,128)(2,1)} %all-gather.10.cloned.1.call-done.refs_1_, ...), custom_call_target="tpu_custom_call" | custom-call | tf_op jit(solution)/shard_map/pair_blocks/pallas_call | solution.py:72
  447.3 6.4 %pair_blocks.4 = bf16[16,128,128]{2,1,0:T(8,128)(2,1)} custom-call(s32[2]{0:T(128)} %pad_add_fusion.1.meta_ref, s32[4,64]{1,0:T(4,128)} %pad_add_fusion.loc_ref, bf16[4096,1024]{1,0:T(8,128)(2,1)} %all-gather.8.cloned.1.call-done.refs_0_, bf16[4096,1024]{1,0:T(8,128)(2,1)} %all-gather.10.cloned.1.call-done.refs_1_, ...), custom_call_target="tpu_custom_call" | custom-call | tf_op jit(solution)/shard_map/pair_blocks/pallas_call | solution.py:72
  453.7 12.3 %collective-permute-done.17 = bf16[16,128,128]{2,1,0:T(8,128)(2,1)S(1)} collective-permute-done((bf16[16,128,128]{2,1,0:T(8,128)(2,1)}, bf16[16,128,128]{2,1,0:T(8,128)(2,1)S(1)}, u32[]{:S(2)}, u32[]{:S(2)}) %collective-permute-start.17) | collective-permute-done | bytes 524320 | tf_op jit(solution)/shard_map/ppermute | solution.py:184
  466.0 13.3 %collective-permute-done.18 = bf16[16,128,128]{2,1,0:T(8,128)(2,1)S(1)} collective-permute-done((bf16[16,128,128]{2,1,0:T(8,128)(2,1)}, bf16[16,128,128]{2,1,0:T(8,128)(2,1)S(1)}, u32[]{:S(2)}, u32[]{:S(2)}) %collective-permute-start.18) | collective-permute-done | bytes 524320 | tf_op jit(solution)/shard_map/ppermute | solution.py:184
  479.3 4.3 fusion
  (104 shorter events, 29.8 us)
Async XLA Ops:
  6.5 472.8 %copy-start = (bf16[128,1024]{1,0:T(8,128)(2,1)S(1)}, bf16[128,1024]{1,0:T(8,128)(2,1)}, u32[]{:S(2)}) copy-start(bf16[128,1024]{1,0:T(8,128)(2,1)} %param.18) | copy-start | bytes 786436
  6.5 87.7 %all-gather.6.cloned.1.call-start = ((), (), s32[]{:S(2)}) async-start(), calls=%async_computation | async-start | bytes 9437184 | tf_op jit(solution)/shard_map/all_gather | solution.py:110
  7.9 26.8 %collective-permute-start.3 = (bf16[128,4096]{1,0:T(8,128)(2,1)S(1)}, bf16[128,4096]{1,0:T(8,128)(2,1)S(1)}, u32[]{:S(2)}, u32[]{:S(2)}) collective-permute-start(bf16[128,4096]{1,0:T(8,128)(2,1)S(1)} %constant_dynamic-slice_fusion.4), channel_id=1, source_target_pairs={{0,8},{24,16},{1,9},{25,17},{2,10},{26,18},{3,11},{27,19},{4,12},{... | collective-permute-start | bytes 3145736 | tf_op jit(solution)/shard_map/ppermute | solution.py:108
  35.8 352.5 %all-gather.14.cloned.1.call-start = ((), (), s32[]{:S(2)}) async-start(), calls=%async_computation.4 | async-start | bytes 9437184 | tf_op jit(solution)/shard_map/all_gather | solution.py:172
  39.6 26.0 %collective-permute-start.13 = (bf16[1024,512]{1,0:T(8,128)(2,1)S(1)}, bf16[1024,512]{1,0:T(8,128)(2,1)}, u32[]{:S(2)}, u32[]{:S(2)}) collective-permute-start(bf16[1024,512]{1,0:T(8,128)(2,1)S(1)} %get-tuple-element.18), channel_id=1, source_target_pairs={{0,8},{24,16},{1,9},{25,17},{2,10},{26,18},{3,11},{27,19},{4,12},{... | collective-permute-start | bytes 3145736 | tf_op jit(solution)/shard_map/ppermute | solution.py:115
  40.9 35.3 %collective-permute-start.14 = (bf16[1024,512]{1,0:T(8,128)(2,1)S(1)}, bf16[1024,512]{1,0:T(8,128)(2,1)}, u32[]{:S(2)}, u32[]{:S(2)}) collective-permute-start(bf16[1024,512]{1,0:T(8,128)(2,1)S(1)} %get-tuple-element.18), channel_id=1, source_target_pairs={{8,16},{16,8},{9,17},{17,9},{10,18},{18,10},{11,19},{19,11},{12,20... | collective-permute-start | bytes 3145736 | tf_op jit(solution)/shard_map/ppermute | solution.py:116
  65.7 25.3 %collective-permute-start.15 = (bf16[1024,512]{1,0:T(8,128)(2,1)}, bf16[1024,512]{1,0:T(8,128)(2,1)S(1)}, u32[]{:S(2)}, u32[]{:S(2)}) collective-permute-start(bf16[1024,512]{1,0:T(8,128)(2,1)} %collective-permute-done.13), channel_id=1, source_target_pairs={{8,16},{16,8},{9,17},{17,9},{10,18},{18,10},{11,19},{19,11},{12,20... | collective-permute-start | bytes 3145736 | tf_op jit(solution)/shard_map/ppermute | solution.py:117
  98.8 14.5 %slice-start = ((s8[8388608]{0:T(1024)(128)(4,1)}), s8[4194304]{0:T(1024)(128)(4,1)S(1)}, s32[]{:S(2)}) async-start(s8[8388608]{0:T(1024)(128)(4,1)} %bitcast.54), calls=%async_computation.5 | async-start | bytes 8388608
  99.6 11.3 %copy-start.1 = (bf16[1024,4096]{1,0:T(8,128)(2,1)}, bf16[1024,4096]{1,0:T(8,128)(2,1)S(1)}, u32[]{:S(2)}) copy-start(bf16[1024,4096]{1,0:T(8,128)(2,1)S(1)} %pad_maximum_fusion.1) | copy-start | bytes 25165828
  99.6 13.7 %slice-start.1 = ((s8[8388608]{0:T(1024)(128)(4,1)}), s8[4194304]{0:T(1024)(128)(4,1)S(1)}, s32[]{:S(2)}) async-start(s8[8388608]{0:T(1024)(128)(4,1)} %bitcast.54), calls=%async_computation.6 | async-start | bytes 8388608
  99.6 13.7 %copy-start.3 = (bf16[4096,512]{1,0:T(8,128)(2,1)S(1)}, bf16[4096,512]{1,0:T(8,128)(2,1)}, u32[]{:S(2)}) copy-start(bf16[4096,512]{1,0:T(8,128)(2,1)} %pad_maximum_fusion.5) | copy-start | bytes 12582916
  110.8 22.9 %collective-permute-start.16 = (bf16[512,1024]{1,0:T(8,128)(2,1)}, bf16[512,1024]{1,0:T(8,128)(2,1)}, u32[]{:S(2)}, u32[]{:S(2)}) collective-permute-start(bf16[512,1024]{1,0:T(8,128)(2,1)} %convolution_convert_fusion), channel_id=1, source_target_pairs={{8,0},{16,24},{9,1},{17,25},{10,2},{18,26},{11,3},{19,27},{12,4},{... | collective-permute-start | bytes 3145736 | tf_op jit(solution)/shard_map/ppermute | solution.py:121
  135.0 253.3 %all-gather.12.cloned.1.call-start = ((), (), s32[]{:S(2)}) async-start(), calls=%async_computation.3 | async-start | bytes 9437184 | tf_op jit(solution)/shard_map/all_gather | solution.py:172
  135.0 52.6 %copy-start.2 = (bf16[1024,4096]{1,0:T(8,128)(2,1)S(1)}, bf16[1024,4096]{1,0:T(8,128)(2,1)}, u32[]{:S(2)}) copy-start(bf16[1024,4096]{1,0:T(8,128)(2,1)} %copy-done.1) | copy-start | bytes 25165828
  135.0 26.7 %collective-permute-start.9 = (bf16[1024,512]{1,0:T(8,128)(2,1)}, bf16[1024,512]{1,0:T(8,128)(2,1)S(1)}, u32[]{:S(2)}, u32[]{:S(2)}) collective-permute-start(bf16[1024,512]{1,0:T(8,128)(2,1)} %get-tuple-element.21), channel_id=1, source_target_pairs={{0,8},{24,16},{1,9},{25,17},{2,10},{26,18},{3,11},{27,19},{4,12},{... | collective-permute-start | bytes 3145736 | tf_op jit(solution)/shard_map/ppermute | solution.py:115
  136.6 27.0 %collective-permute-start.10 = (bf16[1024,512]{1,0:T(8,128)(2,1)}, bf16[1024,512]{1,0:T(8,128)(2,1)S(1)}, u32[]{:S(2)}, u32[]{:S(2)}) collective-permute-start(bf16[1024,512]{1,0:T(8,128)(2,1)} %get-tuple-element.21), channel_id=1, source_target_pairs={{8,16},{16,8},{9,17},{17,9},{10,18},{18,10},{11,19},{19,11},{12,20... | collective-permute-start | bytes 3145736 | tf_op jit(solution)/shard_map/ppermute | solution.py:116
  161.7 24.4 %collective-permute-start.11 = (bf16[1024,512]{1,0:T(8,128)(2,1)S(1)}, bf16[1024,512]{1,0:T(8,128)(2,1)S(1)}, u32[]{:S(2)}, u32[]{:S(2)}) collective-permute-start(bf16[1024,512]{1,0:T(8,128)(2,1)S(1)} %collective-permute-done.9), channel_id=1, source_target_pairs={{8,16},{16,8},{9,17},{17,9},{10,18},{18,10},{11,19},{19,11},{12,20... | collective-permute-start | bytes 3145736 | tf_op jit(solution)/shard_map/ppermute | solution.py:117
  186.1 8.6 %slice-start.2 = ((s8[8388608]{0:T(1024)(128)(4,1)}), s8[4194304]{0:T(1024)(128)(4,1)S(1)}, s32[]{:S(2)}) async-start(s8[8388608]{0:T(1024)(128)(4,1)} %bitcast.56), calls=%async_computation.7 | async-start | bytes 8388608
  187.6 7.1 %slice-start.3 = ((s8[8388608]{0:T(1024)(128)(4,1)}), s8[4194304]{0:T(1024)(128)(4,1)S(1)}, s32[]{:S(2)}) async-start(s8[8388608]{0:T(1024)(128)(4,1)} %bitcast.56), calls=%async_computation.8 | async-start | bytes 8388608
  193.2 21.1 %collective-permute-start.12 = (bf16[512,1024]{1,0:T(8,128)(2,1)}, bf16[512,1024]{1,0:T(8,128)(2,1)S(1)}, u32[]{:S(2)}, u32[]{:S(2)}) collective-permute-start(bf16[512,1024]{1,0:T(8,128)(2,1)} %convolution_convert_fusion.2), channel_id=1, source_target_pairs={{8,0},{16,24},{9,1},{17,25},{10,2},{18,26},{11,3},{19,27},{12,4},{... | collective-permute-start | bytes 3145736 | tf_op jit(solution)/shard_map/ppermute | solution.py:121
  215.4 172.8 %all-gather.10.cloned.1.call-start = ((), (), s32[]{:S(2)}) async-start(), calls=%async_computation.2 | async-start | bytes 9437184 | tf_op jit(solution)/shard_map/all_gather | solution.py:172
  215.5 23.3 %collective-permute-start.5 = (bf16[1024,512]{1,0:T(8,128)(2,1)}, bf16[1024,512]{1,0:T(8,128)(2,1)S(1)}, u32[]{:S(2)}, u32[]{:S(2)}) collective-permute-start(bf16[1024,512]{1,0:T(8,128)(2,1)} %get-tuple-element.19), channel_id=1, source_target_pairs={{0,8},{24,16},{1,9},{25,17},{2,10},{26,18},{3,11},{27,19},{4,12},{... | collective-permute-start | bytes 3145736 | tf_op jit(solution)/shard_map/ppermute | solution.py:115
  216.8 24.8 %collective-permute-start.6 = (bf16[1024,512]{1,0:T(8,128)(2,1)}, bf16[1024,512]{1,0:T(8,128)(2,1)S(1)}, u32[]{:S(2)}, u32[]{:S(2)}) collective-permute-start(bf16[1024,512]{1,0:T(8,128)(2,1)} %get-tuple-element.19), channel_id=1, source_target_pairs={{8,16},{16,8},{9,17},{17,9},{10,18},{18,10},{11,19},{19,11},{12,20... | collective-permute-start | bytes 3145736 | tf_op jit(solution)/shard_map/ppermute | solution.py:116
  238.8 23.8 %collective-permute-start.7 = (bf16[1024,512]{1,0:T(8,128)(2,1)S(1)}, bf16[1024,512]{1,0:T(8,128)(2,1)S(1)}, u32[]{:S(2)}, u32[]{:S(2)}) collective-permute-start(bf16[1024,512]{1,0:T(8,128)(2,1)S(1)} %collective-permute-done.5), channel_id=1, source_target_pairs={{8,16},{16,8},{9,17},{17,9},{10,18},{18,10},{11,19},{19,11},{12,20... | collective-permute-start | bytes 3145736 | tf_op jit(solution)/shard_map/ppermute | solution.py:117
  262.5 10.8 %slice-start.4 = ((s8[8388608]{0:T(1024)(128)(4,1)}), s8[4194304]{0:T(1024)(128)(4,1)S(1)}, s32[]{:S(2)}) async-start(s8[8388608]{0:T(1024)(128)(4,1)} %bitcast.58), calls=%async_computation.9 | async-start | bytes 8388608
  264.1 9.2 %slice-start.5 = ((s8[8388608]{0:T(1024)(128)(4,1)}), s8[4194304]{0:T(1024)(128)(4,1)S(1)}, s32[]{:S(2)}) async-start(s8[8388608]{0:T(1024)(128)(4,1)} %bitcast.58), calls=%async_computation.10 | async-start | bytes 8388608
  271.5 20.2 %collective-permute-start.8 = (bf16[512,1024]{1,0:T(8,128)(2,1)S(1)}, bf16[512,1024]{1,0:T(8,128)(2,1)S(1)}, u32[]{:S(2)}, u32[]{:S(2)}) collective-permute-start(bf16[512,1024]{1,0:T(8,128)(2,1)S(1)} %convolution_convert_fusion.4), channel_id=1, source_target_pairs={{8,0},{16,24},{9,1},{17,25},{10,2},{18,26},{11,3},{19,27},{12,4},{... | collective-permute-start | bytes 3145736 | tf_op jit(solution)/shard_map/ppermute | solution.py:121
  292.8 131.0 %all-gather.8.cloned.1.call-start = ((), (), s32[]{:S(2)}) async-start(), calls=%async_computation.1 | async-start | bytes 9437184 | tf_op jit(solution)/shard_map/all_gather | solution.py:172
  292.9 22.6 %collective-permute-start = (bf16[1024,512]{1,0:T(8,128)(2,1)S(1)}, bf16[1024,512]{1,0:T(8,128)(2,1)S(1)}, u32[]{:S(2)}, u32[]{:S(2)}) collective-permute-start(bf16[1024,512]{1,0:T(8,128)(2,1)S(1)} %get-tuple-element.20), channel_id=1, source_target_pairs={{0,8},{24,16},{1,9},{25,17},{2,10},{26,18},{3,11},{27,19},{4,12},{... | collective-permute-start | bytes 3145736 | tf_op jit(solution)/shard_map/ppermute | solution.py:115
  294.2 24.3 %collective-permute-start.1 = (bf16[1024,512]{1,0:T(8,128)(2,1)S(1)}, bf16[1024,512]{1,0:T(8,128)(2,1)S(1)}, u32[]{:S(2)}, u32[]{:S(2)}) collective-permute-start(bf16[1024,512]{1,0:T(8,128)(2,1)S(1)} %get-tuple-element.20), channel_id=1, source_target_pairs={{8,16},{16,8},{9,17},{17,9},{10,18},{18,10},{11,19},{19,11},{12,20... | collective-permute-start | bytes 3145736 | tf_op jit(solution)/shard_map/ppermute | solution.py:116
  315.5 23.6 %collective-permute-start.2 = (bf16[1024,512]{1,0:T(8,128)(2,1)S(1)}, bf16[1024,512]{1,0:T(8,128)(2,1)S(1)}, u32[]{:S(2)}, u32[]{:S(2)}) collective-permute-start(bf16[1024,512]{1,0:T(8,128)(2,1)S(1)} %collective-permute-done), channel_id=1, source_target_pairs={{8,16},{16,8},{9,17},{17,9},{10,18},{18,10},{11,19},{19,11},{12,20... | collective-permute-start | bytes 3145736 | tf_op jit(solution)/shard_map/ppermute | solution.py:117
  339.1 9.5 %slice-start.6 = ((s8[8388608]{0:T(1024)(128)(4,1)}), s8[4194304]{0:T(1024)(128)(4,1)S(1)}, s32[]{:S(2)}) async-start(s8[8388608]{0:T(1024)(128)(4,1)} %bitcast.60), calls=%async_computation.11 | async-start | bytes 8388608
  339.4 9.2 %slice-start.7 = ((s8[8388608]{0:T(1024)(128)(4,1)}), s8[4194304]{0:T(1024)(128)(4,1)S(1)}, s32[]{:S(2)}) async-start(s8[8388608]{0:T(1024)(128)(4,1)} %bitcast.60), calls=%async_computation.12 | async-start | bytes 8388608
  346.9 22.2 %copy-start.5 = (s32[1,8,16]{2,1,0:T(8,128)S(1)}, s32[1,8,16]{2,1,0:T(8,128)}, u32[]{:S(2)}) copy-start(s32[1,8,16]{2,1,0:T(8,128)} %param.13) | copy-start | bytes 1540
  346.9 22.4 %copy-start.6 = (s32[1,128]{1,0:T(1,128)S(1)}, s32[1,128]{1,0:T(1,128)}, u32[]{:S(2)}) copy-start(s32[1,128]{1,0:T(1,128)} %param.14) | copy-start | bytes 1540
  346.9 25.5 %copy-start.8 = (u32[32]{0:T(128)S(1)}, u32[32]{0:T(128)}, u32[]{:S(2)}) copy-start(u32[32]{0:T(128)} %constant.145) | copy-start | bytes 388
  346.9 26.7 %copy-start.7 = (bf16[16]{0:T(256)(128)(2,1)S(1)}, bf16[16]{0:T(256)(128)(2,1)}, u32[]{:S(2)}) copy-start(bf16[16]{0:T(256)(128)(2,1)} %param.16) | copy-start | bytes 100
  346.9 20.4 %collective-permute-start.4 = (bf16[512,1024]{1,0:T(8,128)(2,1)S(1)}, bf16[512,1024]{1,0:T(8,128)(2,1)S(1)}, u32[]{:S(2)}, u32[]{:S(2)}) collective-permute-start(bf16[512,1024]{1,0:T(8,128)(2,1)S(1)} %convolution_convert_fusion.6), channel_id=1, source_target_pairs={{8,0},{16,24},{9,1},{17,25},{10,2},{18,26},{11,3},{19,27},{12,4},{... | collective-permute-start | bytes 3145736 | tf_op jit(solution)/shard_map/ppermute | solution.py:121
  430.6 35.5 %collective-permute-start.17 = (bf16[16,128,128]{2,1,0:T(8,128)(2,1)}, bf16[16,128,128]{2,1,0:T(8,128)(2,1)S(1)}, u32[]{:S(2)}, u32[]{:S(2)}) collective-permute-start(bf16[16,128,128]{2,1,0:T(8,128)(2,1)} %pair_blocks.5), channel_id=1, source_target_pairs={{0,16},{8,24},{16,0},{24,8},{1,17},{9,25},{17,1},{25,9},{2,18},{10... | collective-permute-start | bytes 1572872 | tf_op jit(solution)/shard_map/ppermute | solution.py:184
  432.6 14.6 %copy-start.4 = (f32[1024]{0:T(1024)S(1)}, f32[1024]{0:T(1024)}, u32[]{:S(2)}) copy-start(f32[1024]{0:T(1024)} %param.17) | copy-start | bytes 12292
  432.6 46.7 %collective-permute-start.18 = (bf16[16,128,128]{2,1,0:T(8,128)(2,1)}, bf16[16,128,128]{2,1,0:T(8,128)(2,1)S(1)}, u32[]{:S(2)}, u32[]{:S(2)}) collective-permute-start(bf16[16,128,128]{2,1,0:T(8,128)(2,1)} %pair_blocks.6), channel_id=1, source_target_pairs={{0,8},{8,16},{16,24},{24,0},{1,9},{9,17},{17,25},{25,1},{2,10},{10... | collective-permute-start | bytes 1572872 | tf_op jit(solution)/shard_map/ppermute | solution.py:184
  445.0 34.3 %collective-permute-start.19 = (bf16[16,128,128]{2,1,0:T(8,128)(2,1)}, bf16[16,128,128]{2,1,0:T(8,128)(2,1)S(1)}, u32[]{:S(2)}, u32[]{:S(2)}) collective-permute-start(bf16[16,128,128]{2,1,0:T(8,128)(2,1)} %pair_blocks.7), channel_id=1, source_target_pairs={{0,24},{8,0},{16,8},{24,16},{1,25},{9,1},{17,9},{25,17},{2,26},{10... | collective-permute-start | bytes 1572872 | tf_op jit(solution)/shard_map/ppermute | solution.py:184
Sparse Core Ops, SparseCore 0:
  35.9 54.2 all-gather.5
  135.1 56.4 all-gather.13
  215.6 55.1 all-gather.11
  293.0 55.2 all-gather.9
  368.5 55.3 all-gather.7
